TPU v7x, 32 devices: a whole 2x2x4 slice. The times are simulated.
32 devices in a mesh: scen: 4 (over x, core), var: 8 (over z, y).
Axes of the slice: x: 2, y: 2, z: 4, core: 2. Of those that a mesh axis runs over, the one named last changes fastest.
Arguments:
- start_point: float32 [512, 65536], P('scen', 'var'), may hold values from -1 to 1
- multipliers: float32 [512, 65536], P('scen', 'var'), may hold values from -3 to 3
- cost: bfloat16 [512, 65536], P('scen', 'var'), may hold values from -6 to 6
- curvature: bfloat16 [512, 65536], P('scen', 'var'), may hold values from 0.5 to 2
- recourse_rhs: float32 [512, 512], P('scen'), may hold values from -12 to 12
- technology: bfloat16 [512, 65536], P(None, 'var'), may hold values from -0.0234375 to 0.0234375
- scenario_weight: float32 [512], P('scen'), may hold values from 1 to 30
- previous_mean: float32 [4, 65536], P(None, 'var'), may hold values from -1 to 1
- active: int32 [512, 512], P('scen', 'var'), may hold values 0 or 1
Outputs:
- iterate: float32 [512, 65536], P('scen', 'var')
- new_multipliers: float32 [512, 65536], P('scen', 'var')
- bundle_mean: float32 [4, 65536], P(None, 'var')
- primal_norm: float32 [], replicated
- dual_norm: float32 [], replicated
All inputs are finite; a program needn't handle non-finite values. No bound on the sum of `active` on one device may be relied on, other than what follows from the above.
Results may differ from a plain program's by a relative error of at most 0.0007.
Values sent between devices are 32-bit elements; how exact they have to be, the bound alone decides.
A program may use at most 64 MiB of HBM per device.

v0:
```python
import jax
import jax.numpy as jnp
from jax import lax
from jax.sharding import PartitionSpec as P

V = 65536
BLK = 128
STEPS = 8
highest = lax.Precision.HIGHEST
penalty = 1.0
recourse_scale = 4.0
stride = 0.2
epsilon = 1e-06


def from_partner(block, axis, bit):
    count = lax.axis_size(axis)
    route = []
    for low in range(count):
        high = low | 1 << bit
        if high != low and high < count:
            route += [(low, high), (high, low)]
    return lax.ppermute(block, axis, route)


def shards(
    start_point,
    multipliers,
    cost,
    curvature,
    recourse_rhs,
    technology,
    scenario_weight,
    previous_mean,
    active,
):
    scen_rows, var_cols = start_point.shape
    groups = previous_mean.shape[0]
    group_size = lax.axis_size("scen") // groups
    position = lax.axis_index("scen")
    my_node = position // group_size
    node_of = jnp.full((scen_rows,), my_node, jnp.int32)
    member = (node_of[:, None] == jnp.arange(groups, dtype=jnp.int32)[None, :]).astype(jnp.float32)
    bundle_mass = lax.psum(jnp.sum(member * scenario_weight[:, None], axis=0), "scen")
    anchor = jnp.dot(member, previous_mean, precision=highest, preferred_element_type=jnp.float32)
    linear = cost.astype(jnp.float32) + multipliers - penalty * anchor
    diagonal = curvature.astype(jnp.float32) + penalty
    active_mask = (active > 0)[:, :, None]
    iterate = start_point
    for sweep in range(STEPS):
        rounded = iterate.astype(jnp.bfloat16)
        partial_image = lax.dot_general(
            rounded, technology, (((1,), (1,)), ((), ())), preferred_element_type=jnp.float32
        )
        image = lax.psum(partial_image, "var")
        shortfall = (image - recourse_rhs).astype(jnp.bfloat16)
        pullback = jnp.dot(shortfall, technology, preferred_element_type=jnp.float32)
        stepped = jnp.clip(
            iterate - stride * (diagonal * iterate + linear + recourse_scale * pullback), -1.0, 1.0
        )
        blocked = jnp.where(
            active_mask, stepped.reshape(scen_rows, -1, BLK), iterate.reshape(scen_rows, -1, BLK)
        )
        iterate = blocked.reshape(scen_rows, var_cols)
    weighted = scenario_weight[:, None] * iterate
    normaliser = jnp.sum(bundle_mass) * V
    own_total = jnp.sum(weighted, axis=0, keepdims=True)
    for bit in range(group_size.bit_length() - 1):
        own_total = own_total + from_partner(own_total, "scen", bit)
    own_mass = jnp.sum(
        bundle_mass * (jnp.arange(groups, dtype=jnp.int32) == my_node).astype(jnp.float32)
    )
    mean_row = own_total / own_mass
    old_row = lax.dynamic_slice_in_dim(previous_mean, my_node, 1, 0)
    leader = (position % group_size == 0).astype(jnp.float32)
    centred = iterate - mean_row
    drift_part = leader * own_mass * jnp.sum((mean_row - old_row) ** 2)
    spread_part = jnp.sum(scenario_weight[:, None] * centred * centred)
    drift_sum, spread = lax.psum((drift_part, spread_part), ("scen", "var"))
    collected = lax.all_gather(mean_row, "scen", axis=0, tiled=True)
    bundle_mean = collected.reshape(groups, group_size, var_cols)[:, 0, :]
    primal_norm = jnp.sqrt(spread / normaliser + epsilon)
    dual_norm = penalty * jnp.sqrt(drift_sum / normaliser + epsilon)
    factor = penalty * jnp.sqrt(primal_norm / dual_norm)
    new_multipliers = multipliers + factor * centred
    return (iterate, new_multipliers, bundle_mean, primal_norm, dual_norm)


def solution(mesh):
    placed = (
        P("scen", "var"),
        P("scen", "var"),
        P("scen", "var"),
        P("scen", "var"),
        P("scen", None),
        P(None, "var"),
        P("scen"),
        P(None, "var"),
        P("scen", "var"),
    )
    return jax.shard_map(
        shards,
        mesh=mesh,
        in_specs=placed,
        out_specs=(P("scen", "var"), P("scen", "var"), P(None, "var"), P(), P()),
        check_vma=False,
    )
```

profile of v0, /device:TPU:0, one launch (start us, length us, event | category | flops | bytes accessed | tf_op | source)
XLA Modules:
  0.0 788.8 jit_solution(14389353718733308539)
XLA Ops:
  7.2 8.3 %fusion.55 = f32[128,512]{1,0:T(8,128)} fusion(bf16[512,8192]{1,0:T(8,128)(2,1)} %param.14, f32[128,8192]{1,0:T(8,128)} %param.9), kind=kOutput, calls=%fused_computation.68 | convolution fusion | flops 1074790400 | bytes 12845056 | tf_op jit(solution)/shard_map/dot_general | solution.py:52
  15.8 6.9 convolution_subtract_fusion
  22.8 66.7 %all-reduce.10.cloned.1.call-done = f32[128,512]{1,0:T(8,128)} async-done(((f32[128,512]{1,0:T(8,128)}), f32[128,512]{1,0:T(8,128)}) %all-reduce.10.cloned.1.call-update) | async-done | bytes 262160 | tf_op jit(solution)/shard_map/psum | solution.py:55
  89.4 2.7 broadcast_in_dim.37
  92.2 9.2 %fusion.39 = f32[128,8192]{1,0:T(8,128)S(1)} fusion(f32[128,8192]{1,0:T(8,128)} %param.9, bf16[512,8192]{1,0:T(8,128)(2,1)} %param.14, f32[128,8192]{1,0:T(8,128)} %convolution_subtract_fusion, bf16[128,8192]{1,0:T(8,128)(2,1)S(1)} %copy-done, f32[128,512]{1,0:T(8,128)} %all-reduce.10.cloned.1.call-done, f32[128,512]{1,0:T(8,128)S(1)} %copy-done.8, ...), kind=kOutput, calls=%fused_computation.48 | convolution fusion | flops 1084358656 | bytes 24641536 | tf_op jit(solution)/shard_map/dot_general | solution.py:57
  101.4 2.0 copy-done.7
  103.4 3.6 fusion.53
  107.3 70.2 %all-reduce.12.cloned.1.call-done = f32[128,512]{1,0:T(8,128)} async-done(((f32[128,512]{1,0:T(8,128)}), f32[128,512]{1,0:T(8,128)}) %all-reduce.12.cloned.1.call-update) | async-done | bytes 262160 | tf_op jit(solution)/shard_map/psum | solution.py:55
  177.5 9.0 %fusion.37 = f32[128,8192]{1,0:T(8,128)S(1)} fusion(f32[128,8192]{1,0:T(8,128)} %copy-done.7, bf16[512,8192]{1,0:T(8,128)(2,1)} %param.14, f32[128,8192]{1,0:T(8,128)} %convolution_subtract_fusion, bf16[128,8192]{1,0:T(8,128)(2,1)S(1)} %copy-done, f32[128,512]{1,0:T(8,128)} %all-reduce.12.cloned.1.call-done, f32[128,512]{1,0:T(8,128)S(1)} %copy-done.8, ...), kind=kOutput, calls=%fused_computation.46 | convolution fusion | flops 1084358656 | bytes 24641536 | tf_op jit(solution)/shard_map/dot_general | solution.py:57
  188.5 7.0 fusion.51
  195.6 70.3 %all-reduce.14.cloned.1.call-done = f32[128,512]{1,0:T(8,128)} async-done(((f32[128,512]{1,0:T(8,128)}), f32[128,512]{1,0:T(8,128)}) %all-reduce.14.cloned.1.call-update) | async-done | bytes 262160 | tf_op jit(solution)/shard_map/psum | solution.py:55
  265.9 9.0 %fusion.35 = f32[128,8192]{1,0:T(8,128)S(1)} fusion(f32[128,8192]{1,0:T(8,128)} %copy-done.2, bf16[512,8192]{1,0:T(8,128)(2,1)} %param.14, f32[128,8192]{1,0:T(8,128)} %convolution_subtract_fusion, bf16[128,8192]{1,0:T(8,128)(2,1)S(1)} %copy-done, f32[128,512]{1,0:T(8,128)} %all-reduce.14.cloned.1.call-done, f32[128,512]{1,0:T(8,128)S(1)} %copy-done.8, ...), kind=kOutput, calls=%fused_computation.44 | convolution fusion | flops 1084358656 | bytes 24641536 | tf_op jit(solution)/shard_map/dot_general | solution.py:57
  277.0 7.0 fusion.49
  284.3 70.1 %all-reduce.16.cloned.1.call-done = f32[128,512]{1,0:T(8,128)} async-done(((f32[128,512]{1,0:T(8,128)}), f32[128,512]{1,0:T(8,128)}) %all-reduce.16.cloned.1.call-update) | async-done | bytes 262160 | tf_op jit(solution)/shard_map/psum | solution.py:55
  354.4 9.0 %fusion.33 = f32[128,8192]{1,0:T(8,128)S(1)} fusion(f32[128,8192]{1,0:T(8,128)} %copy-done.3, bf16[512,8192]{1,0:T(8,128)(2,1)} %param.14, f32[128,8192]{1,0:T(8,128)} %convolution_subtract_fusion, bf16[128,8192]{1,0:T(8,128)(2,1)S(1)} %copy-done, f32[128,512]{1,0:T(8,128)} %all-reduce.16.cloned.1.call-done, f32[128,512]{1,0:T(8,128)S(1)} %copy-done.8, ...), kind=kOutput, calls=%fused_computation.42 | convolution fusion | flops 1084358656 | bytes 24641536 | tf_op jit(solution)/shard_map/dot_general | solution.py:57
  365.4 7.0 fusion.47
  372.5 70.4 %all-reduce.18.cloned.1.call-done = f32[128,512]{1,0:T(8,128)} async-done(((f32[128,512]{1,0:T(8,128)}), f32[128,512]{1,0:T(8,128)}) %all-reduce.18.cloned.1.call-update) | async-done | bytes 262160 | tf_op jit(solution)/shard_map/psum | solution.py:55
  442.9 9.0 %fusion.31 = f32[128,8192]{1,0:T(8,128)S(1)} fusion(f32[128,8192]{1,0:T(8,128)} %copy-done.4, bf16[512,8192]{1,0:T(8,128)(2,1)} %param.14, f32[128,8192]{1,0:T(8,128)} %convolution_subtract_fusion, bf16[128,8192]{1,0:T(8,128)(2,1)S(1)} %copy-done, f32[128,512]{1,0:T(8,128)} %all-reduce.18.cloned.1.call-done, f32[128,512]{1,0:T(8,128)S(1)} %copy-done.8, ...), kind=kOutput, calls=%fused_computation.40 | convolution fusion | flops 1084358656 | bytes 24641536 | tf_op jit(solution)/shard_map/dot_general | solution.py:57
  453.9 7.0 fusion.45
  461.4 69.9 %all-reduce.20.cloned.1.call-done = f32[128,512]{1,0:T(8,128)} async-done(((f32[128,512]{1,0:T(8,128)}), f32[128,512]{1,0:T(8,128)}) %all-reduce.20.cloned.1.call-update) | async-done | bytes 262160 | tf_op jit(solution)/shard_map/psum | solution.py:55
  531.4 9.0 %fusion.29 = f32[128,8192]{1,0:T(8,128)S(1)} fusion(f32[128,8192]{1,0:T(8,128)} %copy-done.5, bf16[512,8192]{1,0:T(8,128)(2,1)} %param.14, f32[128,8192]{1,0:T(8,128)} %convolution_subtract_fusion, bf16[128,8192]{1,0:T(8,128)(2,1)S(1)} %copy-done, f32[128,512]{1,0:T(8,128)} %all-reduce.20.cloned.1.call-done, f32[128,512]{1,0:T(8,128)S(1)} %copy-done.8, ...), kind=kOutput, calls=%fused_computation.38 | convolution fusion | flops 1084358656 | bytes 24641536 | tf_op jit(solution)/shard_map/dot_general | solution.py:57
  542.4 7.0 fusion.43
  549.5 70.3 %all-reduce.22.cloned.1.call-done = f32[128,512]{1,0:T(8,128)} async-done(((f32[128,512]{1,0:T(8,128)}), f32[128,512]{1,0:T(8,128)}) %all-reduce.22.cloned.1.call-update) | async-done | bytes 262160 | tf_op jit(solution)/shard_map/psum | solution.py:55
  619.8 9.0 %fusion.27 = f32[128,8192]{1,0:T(8,128)S(1)} fusion(f32[128,8192]{1,0:T(8,128)} %copy-done.6, bf16[512,8192]{1,0:T(8,128)(2,1)} %param.14, f32[128,8192]{1,0:T(8,128)} %convolution_subtract_fusion, bf16[128,8192]{1,0:T(8,128)(2,1)S(1)} %copy-done, f32[128,512]{1,0:T(8,128)} %all-reduce.22.cloned.1.call-done, f32[128,512]{1,0:T(8,128)S(1)} %copy-done.8, ...), kind=kOutput, calls=%fused_computation.36 | convolution fusion | flops 1084358656 | bytes 24641536 | tf_op jit(solution)/shard_map/dot_general | solution.py:57
  630.8 7.0 fusion.41
  638.1 5.8 psum.85
  645.2 63.1 %all-reduce.24.cloned.1.call-done = f32[128,512]{1,0:T(8,128)} async-done(((f32[128,512]{1,0:T(8,128)}), f32[128,512]{1,0:T(8,128)}) %all-reduce.24.cloned.1.call-update) | async-done | bytes 262160 | tf_op jit(solution)/shard_map/psum | solution.py:55
  708.3 11.2 %multiply_reduce_fusion = (f32[8192]{0:T(1024)S(1)}, f32[128,8192]{1,0:T(8,128)}) fusion(f32[128]{0:T(128)S(1)} %copy-done.11, f32[128,8192]{1,0:T(8,128)} %copy-done.1, bf16[512,8192]{1,0:T(8,128)(2,1)} %param.14, f32[128,512]{1,0:T(8,128)} %all-reduce.24.cloned.1.call-done, f32[128,512]{1,0:T(8,128)S(1)} %copy-done.8, ...), kind=kOutput, calls=%fused_computation.52 | convolution fusion | flops 1086447616 | bytes 24674816 | tf_op jit(solution)/shard_map/dot_general | solution.py:57
  722.1 3.9 fusion.40
  726.1 5.4 all-gather
  731.5 39.7 %all-reduce = (f32[]{:T(128)}, f32[]{:T(128)}) all-reduce(f32[]{:T(128)} %fusion.40, f32[]{:T(128)S(6)} %mul.145), channel_id=1, replica_groups=mesh['scen'=4,'var'=8] {'scen','var'}, use_global_device_ids=true, to_apply=%region_13.14 | all-reduce | flops 2 | bytes 16 | tf_op jit(solution)/shard_map/psum | solution.py:79
  772.7 6.1 multiply_add_fusion
  (53 shorter events, 16.3 us)
Async XLA Ops:
  7.2 8.5 %copy-start.10 = (s32[128,64]{0,1:T(8,128)S(1)}, s32[128,64]{0,1:T(8,128)}, u32[]{:S(2)}) copy-start(s32[128,64]{0,1:T(8,128)} %param.17) | copy-start | bytes 98308
  7.2 8.6 %copy-start.9 = (f32[4,8192]{1,0:T(4,128)S(1)}, f32[4,8192]{1,0:T(4,128)}, u32[]{:S(2)}) copy-start(f32[4,8192]{1,0:T(4,128)} %param.16) | copy-start | bytes 393220
  7.2 82.3 %all-reduce.10.cloned.1.call-start = ((), (), s32[]{:S(2)}) async-start(), calls=%async_computation | async-start | bytes 524288 | tf_op jit(solution)/shard_map/psum | solution.py:55
  15.6 161.9 %all-reduce.12.cloned.1.call-start = ((), (), s32[]{:S(2)}) async-start(), calls=%async_computation.1 | async-start | bytes 524288 | tf_op jit(solution)/shard_map/psum | solution.py:55
  15.8 76.4 %copy-start = (bf16[128,8192]{1,0:T(8,128)(2,1)S(1)}, bf16[128,8192]{1,0:T(8,128)(2,1)}, u32[]{:S(2)}) copy-start(bf16[128,8192]{1,0:T(8,128)(2,1)} %param.12) | copy-start | bytes 6291460
  15.8 76.4 %copy-start.8 = (f32[128,512]{1,0:T(8,128)S(1)}, f32[128,512]{1,0:T(8,128)}, u32[]{:S(2)}) copy-start(f32[128,512]{1,0:T(8,128)} %param.13) | copy-start | bytes 786436
  89.4 14.0 %slice-start = ((s8[8388608]{0:T(1024)(128)(4,1)}), s8[4194304]{0:T(1024)(128)(4,1)S(1)}, s32[]{:S(2)}) async-start(s8[8388608]{0:T(1024)(128)(4,1)} %bitcast.28), calls=%async_computation.8 | async-start | bytes 8388608
  92.2 11.2 %slice-start.1 = ((s8[8388608]{0:T(1024)(128)(4,1)}), s8[4194304]{0:T(1024)(128)(4,1)S(1)}, s32[]{:S(2)}) async-start(s8[8388608]{0:T(1024)(128)(4,1)} %bitcast.28), calls=%async_computation.9 | async-start | bytes 8388608
  101.4 2.0 copy-start.7
  107.1 158.9 %all-reduce.14.cloned.1.call-start = ((), (), s32[]{:S(2)}) async-start(), calls=%async_computation.2 | async-start | bytes 524288 | tf_op jit(solution)/shard_map/psum | solution.py:55
  186.5 2.0 copy-start.2
  195.6 158.8 %all-reduce.16.cloned.1.call-start = ((), (), s32[]{:S(2)}) async-start(), calls=%async_computation.3 | async-start | bytes 524288 | tf_op jit(solution)/shard_map/psum | solution.py:55
  274.9 2.0 copy-start.3
  284.0 158.9 %all-reduce.18.cloned.1.call-start = ((), (), s32[]{:S(2)}) async-start(), calls=%async_computation.4 | async-start | bytes 524288 | tf_op jit(solution)/shard_map/psum | solution.py:55
  363.4 2.0 copy-start.4
  372.5 158.9 %all-reduce.20.cloned.1.call-start = ((), (), s32[]{:S(2)}) async-start(), calls=%async_computation.5 | async-start | bytes 524288 | tf_op jit(solution)/shard_map/psum | solution.py:55
  451.9 2.0 copy-start.5
  461.0 158.8 %all-reduce.22.cloned.1.call-start = ((), (), s32[]{:S(2)}) async-start(), calls=%async_computation.6 | async-start | bytes 524288 | tf_op jit(solution)/shard_map/psum | solution.py:55
  540.4 2.0 copy-start.6
  549.4 158.8 %all-reduce.24.cloned.1.call-start = ((), (), s32[]{:S(2)}) async-start(), calls=%async_computation.7 | async-start | bytes 524288 | tf_op jit(solution)/shard_map/psum | solution.py:55
  628.8 2.0 copy-start.1
  630.8 7.1 copy-start.11
Sparse Core Ops, SparseCore 0:
  15.7 73.7 all-reduce.9
  107.2 70.2 all-reduce.11
  195.7 70.1 all-reduce.13
  284.1 70.2 all-reduce.15
  372.6 70.2 all-reduce.17
  461.1 70.2 all-reduce.19
  549.6 70.1 all-reduce.21
  638.0 70.2 all-reduce.23
where the time goes:
time: 796 us; the launch traced here: 789 us
  waiting for transfers between devices  551 us (69%)
  matrix products  135 us (17%)
  blocking collectives  50.9 us (6%)
  between operations  20.3 us (3%)
  local copies, waits for them, and re-layouts  17.6 us (2%)
  other arithmetic  12.2 us (2%)
    psum x8, waiting for transfers between devices, shards(): image = lax.psum(partial_image, 'var')  551 us
    dot_general x8, matrix products, shards(): jnp.dot(shortfall, technology, preferred_element_type=jnp.float32)  74.5 us
    dot_general x8, matrix products, shards(): lax.dot_general(rounded, technology, (((1,), (1,)), ((), ())), preferred_...  54 us
    psum x1, blocking collectives, shards(): drift_sum, spread = lax.psum((drift_part, spread_part), ('scen', 'var'))  39.7 us
  transfers between devices with their start and end apart: 8, of which 8 were waited for; matrix products, arithmetic and copies ran while one was open for 1% of the time, Pallas kernels for 0%

commit v1 on v0

--- a/solution.py
+++ b/solution.py
@@ -52,7 +52,7 @@
         partial_image = lax.dot_general(
             rounded, technology, (((1,), (1,)), ((), ())), preferred_element_type=jnp.float32
         )
-        image = lax.psum(partial_image, "var")
+        image = jnp.sum(lax.all_gather(partial_image, "var"), axis=0)
         shortfall = (image - recourse_rhs).astype(jnp.bfloat16)
         pullback = jnp.dot(shortfall, technology, preferred_element_type=jnp.float32)
         stepped = jnp.clip(

time: 796 us -> 637 us (0.80)
  waiting for transfers between devices: 551 us -> 372 us
  other arithmetic: 12.2 us -> 32.5 us
    psum x8 -> x0, waiting for transfers between devices: 551 us -> none  [shards(): image = lax.psum(partial_image, 'var')]
    all_gather x0 -> x8, waiting for transfers between devices: none -> 372 us  [shards(): image = jnp.sum(lax.all_gather(partial_image, 'var'), axis=0)]
    reduce_sum x0 -> x8, other arithmetic: none -> 20.3 us  [shards(): image = jnp.sum(lax.all_gather(partial_image, 'var'), axis=0)]
where the time goes in v1:
time: 637 us; the launch traced here: 629 us
  waiting for transfers between devices  372 us (58%)
  matrix products  135 us (21%)
  blocking collectives  50.6 us (8%)
  other arithmetic  32.5 us (5%)
  between operations  20.3 us (3%)
  local copies, waits for them, and re-layouts  17.7 us (3%)
    all_gather x8, waiting for transfers between devices, shards(): image = jnp.sum(lax.all_gather(partial_image, 'var'), axis=0)  372 us
    dot_general x8, matrix products, shards(): jnp.dot(shortfall, technology, preferred_element_type=jnp.float32)  74.5 us
    dot_general x8, matrix products, shards(): lax.dot_general(rounded, technology, (((1,), (1,)), ((), ())), preferred_...  54.3 us
    psum x1, blocking collectives, shards(): drift_sum, spread = lax.psum((drift_part, spread_part), ('scen', 'var'))  39.4 us
    reduce_sum x8, other arithmetic, shards(): image = jnp.sum(lax.all_gather(partial_image, 'var'), axis=0)  20.3 us
    unnamed x30, local copies, waits for them, and re-layouts  14.1 us
  transfers between devices with their start and end apart: 8, of which 8 were waited for; matrix products, arithmetic and copies ran while one was open for 1% of the time, Pallas kernels for 0%

profile of v1, /device:TPU:0, one launch (start us, length us, event | category | flops | bytes accessed | tf_op | source)
XLA Modules:
  0.0 628.8 jit_solution(12343671361552543720)
XLA Ops:
  7.2 8.4 %fusion.55 = f32[128,512]{1,0:T(8,128)} fusion(bf16[512,8192]{1,0:T(8,128)(2,1)} %param.14, f32[128,8192]{1,0:T(8,128)} %param.9), kind=kOutput, calls=%fused_computation.68 | convolution fusion | flops 1074790400 | bytes 12845056 | tf_op jit(solution)/shard_map/dot_general | solution.py:52
  15.9 6.2 convolution_subtract_fusion
  22.1 45.6 %all-gather.18.cloned.1.call-done = f32[1024,512]{1,0:T(8,128)} async-done(((f32[128,512]{1,0:T(8,128)}), f32[1024,512]{1,0:T(8,128)}) %all-gather.18.cloned.1.call-update) | async-done | bytes 2097168 | tf_op jit(solution)/shard_map/all_gather | solution.py:55
  70.2 2.7 broadcast_in_dim.37
  73.0 9.2 %fusion.39 = f32[128,8192]{1,0:T(8,128)S(1)} fusion(f32[128,8192]{1,0:T(8,128)} %param.9, bf16[512,8192]{1,0:T(8,128)(2,1)} %param.14, f32[128,8192]{1,0:T(8,128)} %convolution_subtract_fusion, bf16[128,8192]{1,0:T(8,128)(2,1)S(1)} %copy-done, f32[128,512]{1,0:T(8,128)} %reduce_sum.126, f32[128,512]{1,0:T(8,128)S(1)} %copy-done.8, ...), kind=kOutput, calls=%fused_computation.48 | convolution fusion | flops 1084358656 | bytes 24641536 | tf_op jit(solution)/shard_map/dot_general | solution.py:57
  84.2 3.7 fusion.53
  88.1 47.6 %all-gather.20.cloned.1.call-done = f32[1024,512]{1,0:T(8,128)} async-done(((f32[128,512]{1,0:T(8,128)}), f32[1024,512]{1,0:T(8,128)}) %all-gather.20.cloned.1.call-update) | async-done | bytes 2097168 | tf_op jit(solution)/shard_map/all_gather | solution.py:55
  135.6 2.5 reduce_sum.127
  138.2 9.0 %fusion.37 = f32[128,8192]{1,0:T(8,128)S(1)} fusion(f32[128,8192]{1,0:T(8,128)} %copy-done.7, bf16[512,8192]{1,0:T(8,128)(2,1)} %param.14, f32[128,8192]{1,0:T(8,128)} %convolution_subtract_fusion, bf16[128,8192]{1,0:T(8,128)(2,1)S(1)} %copy-done, f32[128,512]{1,0:T(8,128)} %reduce_sum.127, f32[128,512]{1,0:T(8,128)S(1)} %copy-done.8, ...), kind=kOutput, calls=%fused_computation.46 | convolution fusion | flops 1084358656 | bytes 24641536 | tf_op jit(solution)/shard_map/dot_general | solution.py:57
  149.2 7.0 %fusion.51 = f32[128,512]{1,0:T(8,128)} fusion(bf16[512,8192]{1,0:T(8,128)(2,1)} %param.14, f32[128,8192]{1,0:T(8,128)S(1)} %fusion.37), kind=kOutput, calls=%fused_computation.64 | convolution fusion | flops 1074790400 | bytes 12845056 | tf_op jit(solution)/shard_map/dot_general | solution.py:52
  156.3 47.7 %all-gather.22.cloned.1.call-done = f32[1024,512]{1,0:T(8,128)} async-done(((f32[128,512]{1,0:T(8,128)}), f32[1024,512]{1,0:T(8,128)}) %all-gather.22.cloned.1.call-update) | async-done | bytes 2097168 | tf_op jit(solution)/shard_map/all_gather | solution.py:55
  206.6 9.0 %fusion.35 = f32[128,8192]{1,0:T(8,128)S(1)} fusion(f32[128,8192]{1,0:T(8,128)} %copy-done.2, bf16[512,8192]{1,0:T(8,128)(2,1)} %param.14, f32[128,8192]{1,0:T(8,128)} %convolution_subtract_fusion, bf16[128,8192]{1,0:T(8,128)(2,1)S(1)} %copy-done, f32[128,512]{1,0:T(8,128)} %reduce_sum.128, f32[128,512]{1,0:T(8,128)S(1)} %copy-done.8, ...), kind=kOutput, calls=%fused_computation.44 | convolution fusion | flops 1084358656 | bytes 24641536 | tf_op jit(solution)/shard_map/dot_general | solution.py:57
  217.6 7.0 %fusion.49 = f32[128,512]{1,0:T(8,128)} fusion(bf16[512,8192]{1,0:T(8,128)(2,1)} %param.14, f32[128,8192]{1,0:T(8,128)S(1)} %fusion.35), kind=kOutput, calls=%fused_computation.62 | convolution fusion | flops 1074790400 | bytes 12845056 | tf_op jit(solution)/shard_map/dot_general | solution.py:52
  224.9 47.5 %all-gather.24.cloned.1.call-done = f32[1024,512]{1,0:T(8,128)} async-done(((f32[128,512]{1,0:T(8,128)}), f32[1024,512]{1,0:T(8,128)}) %all-gather.24.cloned.1.call-update) | async-done | bytes 2097168 | tf_op jit(solution)/shard_map/all_gather | solution.py:55
  275.0 9.0 %fusion.33 = f32[128,8192]{1,0:T(8,128)S(1)} fusion(f32[128,8192]{1,0:T(8,128)} %copy-done.3, bf16[512,8192]{1,0:T(8,128)(2,1)} %param.14, f32[128,8192]{1,0:T(8,128)} %convolution_subtract_fusion, bf16[128,8192]{1,0:T(8,128)(2,1)S(1)} %copy-done, f32[128,512]{1,0:T(8,128)} %reduce_sum.129, f32[128,512]{1,0:T(8,128)S(1)} %copy-done.8, ...), kind=kOutput, calls=%fused_computation.42 | convolution fusion | flops 1084358656 | bytes 24641536 | tf_op jit(solution)/shard_map/dot_general | solution.py:57
  286.0 7.0 %fusion.47 = f32[128,512]{1,0:T(8,128)} fusion(bf16[512,8192]{1,0:T(8,128)(2,1)} %param.14, f32[128,8192]{1,0:T(8,128)S(1)} %fusion.33), kind=kOutput, calls=%fused_computation.60 | convolution fusion | flops 1074790400 | bytes 12845056 | tf_op jit(solution)/shard_map/dot_general | solution.py:52
  293.1 47.7 %all-gather.26.cloned.1.call-done = f32[1024,512]{1,0:T(8,128)} async-done(((f32[128,512]{1,0:T(8,128)}), f32[1024,512]{1,0:T(8,128)}) %all-gather.26.cloned.1.call-update) | async-done | bytes 2097168 | tf_op jit(solution)/shard_map/all_gather | solution.py:55
  343.4 9.0 %fusion.31 = f32[128,8192]{1,0:T(8,128)S(1)} fusion(f32[128,8192]{1,0:T(8,128)} %copy-done.4, bf16[512,8192]{1,0:T(8,128)(2,1)} %param.14, f32[128,8192]{1,0:T(8,128)} %convolution_subtract_fusion, bf16[128,8192]{1,0:T(8,128)(2,1)S(1)} %copy-done, f32[128,512]{1,0:T(8,128)} %reduce_sum.130, f32[128,512]{1,0:T(8,128)S(1)} %copy-done.8, ...), kind=kOutput, calls=%fused_computation.40 | convolution fusion | flops 1084358656 | bytes 24641536 | tf_op jit(solution)/shard_map/dot_general | solution.py:57
  354.5 7.0 %fusion.45 = f32[128,512]{1,0:T(8,128)} fusion(bf16[512,8192]{1,0:T(8,128)(2,1)} %param.14, f32[128,8192]{1,0:T(8,128)S(1)} %fusion.31), kind=kOutput, calls=%fused_computation.58 | convolution fusion | flops 1074790400 | bytes 12845056 | tf_op jit(solution)/shard_map/dot_general | solution.py:52
  362.0 47.3 %all-gather.28.cloned.1.call-done = f32[1024,512]{1,0:T(8,128)} async-done(((f32[128,512]{1,0:T(8,128)}), f32[1024,512]{1,0:T(8,128)}) %all-gather.28.cloned.1.call-update) | async-done | bytes 2097168 | tf_op jit(solution)/shard_map/all_gather | solution.py:55
  411.8 9.0 %fusion.29 = f32[128,8192]{1,0:T(8,128)S(1)} fusion(f32[128,8192]{1,0:T(8,128)} %copy-done.5, bf16[512,8192]{1,0:T(8,128)(2,1)} %param.14, f32[128,8192]{1,0:T(8,128)} %convolution_subtract_fusion, bf16[128,8192]{1,0:T(8,128)(2,1)S(1)} %copy-done, f32[128,512]{1,0:T(8,128)} %reduce_sum.131, f32[128,512]{1,0:T(8,128)S(1)} %copy-done.8, ...), kind=kOutput, calls=%fused_computation.38 | convolution fusion | flops 1084358656 | bytes 24641536 | tf_op jit(solution)/shard_map/dot_general | solution.py:57
  422.9 7.0 %fusion.43 = f32[128,512]{1,0:T(8,128)} fusion(bf16[512,8192]{1,0:T(8,128)(2,1)} %param.14, f32[128,8192]{1,0:T(8,128)S(1)} %fusion.29), kind=kOutput, calls=%fused_computation.56 | convolution fusion | flops 1074790400 | bytes 12845056 | tf_op jit(solution)/shard_map/dot_general | solution.py:52
  430.0 47.7 %all-gather.30.cloned.1.call-done = f32[1024,512]{1,0:T(8,128)} async-done(((f32[128,512]{1,0:T(8,128)}), f32[1024,512]{1,0:T(8,128)}) %all-gather.30.cloned.1.call-update) | async-done | bytes 2097168 | tf_op jit(solution)/shard_map/all_gather | solution.py:55
  480.3 9.0 %fusion.27 = f32[128,8192]{1,0:T(8,128)S(1)} fusion(f32[128,8192]{1,0:T(8,128)} %copy-done.6, bf16[512,8192]{1,0:T(8,128)(2,1)} %param.14, f32[128,8192]{1,0:T(8,128)} %convolution_subtract_fusion, bf16[128,8192]{1,0:T(8,128)(2,1)S(1)} %copy-done, f32[128,512]{1,0:T(8,128)} %reduce_sum.132, f32[128,512]{1,0:T(8,128)S(1)} %copy-done.8, ...), kind=kOutput, calls=%fused_computation.36 | convolution fusion | flops 1084358656 | bytes 24641536 | tf_op jit(solution)/shard_map/dot_general | solution.py:57
  491.3 7.0 %fusion.41 = f32[128,512]{1,0:T(8,128)} fusion(bf16[512,8192]{1,0:T(8,128)(2,1)} %param.14, f32[128,8192]{1,0:T(8,128)S(1)} %fusion.27), kind=kOutput, calls=%fused_computation.54 | convolution fusion | flops 1074790400 | bytes 12845056 | tf_op jit(solution)/shard_map/dot_general | solution.py:52
  498.6 5.8 psum.21
  505.7 40.5 %all-gather.32.cloned.1.call-done = f32[1024,512]{1,0:T(8,128)} async-done(((f32[128,512]{1,0:T(8,128)}), f32[1024,512]{1,0:T(8,128)}) %all-gather.32.cloned.1.call-update) | async-done | bytes 2097168 | tf_op jit(solution)/shard_map/all_gather | solution.py:55
  548.7 11.2 %multiply_reduce_fusion = (f32[8192]{0:T(1024)S(1)}, f32[128,8192]{1,0:T(8,128)}) fusion(f32[128]{0:T(128)S(1)} %copy-done.12, f32[128,8192]{1,0:T(8,128)} %copy-done.1, bf16[512,8192]{1,0:T(8,128)(2,1)} %param.14, f32[128,512]{1,0:T(8,128)} %reduce_sum.133, f32[128,512]{1,0:T(8,128)S(1)} %copy-done.8, f32[128,8192]{1,0:T(8,128)} %convolution_subtract_fusion, ...), kind=kOutput, calls=%fused_computation.52 | convolution fusion | flops 1086447616 | bytes 24674816 | tf_op jit(solution)/shard_map/dot_general | solution.py:57
  562.5 3.9 fusion.40
  566.5 5.4 all-gather.8
  571.9 39.4 %all-reduce = (f32[]{:T(128)}, f32[]{:T(128)}) all-reduce(f32[]{:T(128)} %fusion.40, f32[]{:T(128)S(6)} %mul.145), channel_id=1, replica_groups=mesh['scen'=4,'var'=8] {'scen','var'}, use_global_device_ids=true, to_apply=%region_13.14 | all-reduce | flops 2 | bytes 16 | tf_op jit(solution)/shard_map/psum | solution.py:79
  612.7 6.1 multiply_add_fusion
  (63 shorter events, 36.1 us)
Async XLA Ops:
  7.2 8.6 %copy-start.11 = (s32[128,64]{0,1:T(8,128)S(1)}, s32[128,64]{0,1:T(8,128)}, u32[]{:S(2)}) copy-start(s32[128,64]{0,1:T(8,128)} %param.17) | copy-start | bytes 98308
  7.2 8.7 %copy-start.9 = (bf16[128,8192]{1,0:T(8,128)(2,1)S(1)}, bf16[128,8192]{1,0:T(8,128)(2,1)}, u32[]{:S(2)}) copy-start(bf16[128,8192]{1,0:T(8,128)(2,1)} %param.11) | copy-start | bytes 6291460
  7.2 8.7 %copy-start.10 = (f32[4,8192]{1,0:T(4,128)S(1)}, f32[4,8192]{1,0:T(4,128)}, u32[]{:S(2)}) copy-start(f32[4,8192]{1,0:T(4,128)} %param.16) | copy-start | bytes 393220
  7.2 60.5 %all-gather.18.cloned.1.call-start = ((), (), s32[]{:S(2)}) async-start(), calls=%async_computation | async-start | bytes 2359296 | tf_op jit(solution)/shard_map/all_gather | solution.py:55
  15.7 119.9 %all-gather.20.cloned.1.call-start = ((), (), s32[]{:S(2)}) async-start(), calls=%async_computation.1 | async-start | bytes 2359296 | tf_op jit(solution)/shard_map/all_gather | solution.py:55
  15.9 57.0 %copy-start.8 = (f32[128,512]{1,0:T(8,128)S(1)}, f32[128,512]{1,0:T(8,128)}, u32[]{:S(2)}) copy-start(f32[128,512]{1,0:T(8,128)} %param.13) | copy-start | bytes 786436
  22.1 50.8 %copy-start = (bf16[128,8192]{1,0:T(8,128)(2,1)S(1)}, bf16[128,8192]{1,0:T(8,128)(2,1)}, u32[]{:S(2)}) copy-start(bf16[128,8192]{1,0:T(8,128)(2,1)} %param.12) | copy-start | bytes 6291460
  70.2 14.0 %slice-start = ((s8[8388608]{0:T(1024)(128)(4,1)}), s8[4194304]{0:T(1024)(128)(4,1)S(1)}, s32[]{:S(2)}) async-start(s8[8388608]{0:T(1024)(128)(4,1)} %bitcast.36), calls=%async_computation.8 | async-start | bytes 8388608
  72.9 11.2 %slice-start.1 = ((s8[8388608]{0:T(1024)(128)(4,1)}), s8[4194304]{0:T(1024)(128)(4,1)S(1)}, s32[]{:S(2)}) async-start(s8[8388608]{0:T(1024)(128)(4,1)} %bitcast.36), calls=%async_computation.9 | async-start | bytes 8388608
  82.1 2.0 copy-start.7
  87.8 116.2 %all-gather.22.cloned.1.call-start = ((), (), s32[]{:S(2)}) async-start(), calls=%async_computation.2 | async-start | bytes 2359296 | tf_op jit(solution)/shard_map/all_gather | solution.py:55
  147.2 2.0 copy-start.2
  156.2 116.2 %all-gather.24.cloned.1.call-start = ((), (), s32[]{:S(2)}) async-start(), calls=%async_computation.3 | async-start | bytes 2359296 | tf_op jit(solution)/shard_map/all_gather | solution.py:55
  215.6 2.0 copy-start.3
  224.7 116.2 %all-gather.26.cloned.1.call-start = ((), (), s32[]{:S(2)}) async-start(), calls=%async_computation.4 | async-start | bytes 2359296 | tf_op jit(solution)/shard_map/all_gather | solution.py:55
  284.0 2.0 copy-start.4
  293.1 116.2 %all-gather.28.cloned.1.call-start = ((), (), s32[]{:S(2)}) async-start(), calls=%async_computation.5 | async-start | bytes 2359296 | tf_op jit(solution)/shard_map/all_gather | solution.py:55
  352.4 2.0 copy-start.5
  361.5 116.2 %all-gather.30.cloned.1.call-start = ((), (), s32[]{:S(2)}) async-start(), calls=%async_computation.6 | async-start | bytes 2359296 | tf_op jit(solution)/shard_map/all_gather | solution.py:55
  420.9 2.0 copy-start.6
  429.9 116.2 %all-gather.32.cloned.1.call-start = ((), (), s32[]{:S(2)}) async-start(), calls=%async_computation.7 | async-start | bytes 2359296 | tf_op jit(solution)/shard_map/all_gather | solution.py:55
  489.3 2.0 copy-start.1
  491.3 7.1 %copy-start.12 = (f32[128]{0:T(128)S(1)}, f32[128]{0:T(128)}, u32[]{:S(2)}) copy-start(f32[128]{0:T(128)} %param.15) | copy-start | bytes 1540
Sparse Core Ops, SparseCore 0:
  15.8 51.8 all-gather.17
  88.0 47.6 all-gather.19
  156.4 47.6 all-gather.21
  224.8 47.6 all-gather.23
  293.2 47.6 all-gather.25
  361.6 47.6 all-gather.27
  430.1 47.6 all-gather.29
  498.5 47.6 all-gather.31
